TPU v7x, 32 devices: a whole 2x2x4 slice. The times are simulated.
32 devices in a mesh: lat: 8 (over y, x, core), lon: 4 (over z).
Axes of the slice: x: 2, y: 2, z: 4, core: 2. Of those that a mesh axis runs over, the one named last changes fastest.
Arguments:
- inputs: bfloat16 [128, 384, 256], P('lat', 'lon'), may hold values from -6 to 6
- first_filter: bfloat16 [3, 3, 256, 256], replicated, may hold values from -0.125 to 0.125
- second_filter: bfloat16 [3, 3, 256, 256], replicated, may hold values from -0.125 to 0.125
- cotangent: bfloat16 [128, 384, 256], P('lat', 'lon'), may hold values from -30 to 30
Outputs:
- input_grad: bfloat16 [128, 384, 256], P('lat', 'lon')
- first_grad: float32 [3, 3, 256, 256], replicated
- second_grad: float32 [3, 3, 256, 256], replicated
All inputs are finite; a program needn't handle non-finite values.
Results may differ from a plain program's by a relative error of at most 0.0061.
Values may be sent and summed in bfloat16 or wider, within the bound.
No kernel may reach another device: no remote copies, remote signals or barrier semaphores. Data moves between devices by JAX's collectives and lax.ppermute only.
A program may use at most 64 MiB of HBM per device.

v0:
```python
import jax
import jax.numpy as jnp
from jax import lax
from jax.sharding import PartitionSpec as P


def extended(block, sides, width):
    for axis, dim in sides:
        count = lax.axis_size(axis)
        forward = [(i, i + 1) for i in range(count - 1)]
        forward.append((count - 1, 0))
        backward = [(target, source) for source, target in forward]
        low = lax.ppermute(
            lax.slice_in_dim(block, block.shape[dim] - width, None, axis=dim), axis, forward
        )
        high = lax.ppermute(lax.slice_in_dim(block, 0, width, axis=dim), axis, backward)
        block = jnp.concatenate([low, block, high], axis=dim)
    return block


def mask_rows(padded, width):
    rows = padded.shape[0] - 2 * width
    position = lax.broadcasted_iota(jnp.int32, (padded.shape[0], 1, 1), 0)
    index = lax.axis_index("lat")
    count = lax.axis_size("lat")
    dropped = (position < width) & (index == 0) | (position >= rows + width) & (index == count - 1)
    return jnp.where(dropped, jnp.zeros((), padded.dtype), padded)


def extend(field):
    padded = extended(field, (("lat", 0), ("lon", 1)), 1)
    return mask_rows(padded, 1)


def conv_taps(padded, weight, rows, cols, flipped):
    total = jnp.zeros(
        (rows * cols, weight.shape[3] if not flipped else weight.shape[2]), jnp.float32
    )
    for first in range(3):
        for second in range(3):
            piece = padded[first : first + rows, second : second + cols, :].reshape(rows * cols, -1)
            if flipped:
                total = total + lax.dot_general(
                    piece,
                    weight[2 - first, 2 - second],
                    (((1,), (1,)), ((), ())),
                    preferred_element_type=jnp.float32,
                )
            else:
                total = total + jnp.dot(
                    piece, weight[first, second], preferred_element_type=jnp.float32
                )
    return total.reshape(rows, cols, -1)


def filter_grad(padded, delta, rows, cols):
    flat = delta.reshape(rows * cols, -1)
    taps = []
    for first in range(3):
        for second in range(3):
            piece = padded[first : first + rows, second : second + cols, :].reshape(rows * cols, -1)
            taps.append(
                lax.dot_general(
                    piece, flat, (((0,), (0,)), ((), ())), preferred_element_type=jnp.float32
                )
            )
    return jnp.stack(taps).reshape(3, 3, flat.shape[1], flat.shape[1])


def gelu_value(value):
    return value * 0.5 * (1.0 + jax.scipy.special.erf(value * 0.7071067811865476))


def gelu_slope(value):
    return (
        0.5 * (1.0 + jax.scipy.special.erf(value * 0.7071067811865476))
        + value * jnp.exp(-0.5 * value * value) * 0.3989422804014327
    )


def body(inputs, first_filter, second_filter, cotangent):
    rows, cols = (inputs.shape[0], inputs.shape[1])
    padded_in = extend(inputs)
    hidden_one = conv_taps(padded_in, first_filter, rows, cols, False)
    act = gelu_value(hidden_one).astype(jnp.bfloat16)
    padded_act = extend(act)
    hidden_two = conv_taps(padded_act, second_filter, rows, cols, False)
    delta_two = (cotangent.astype(jnp.float32) * gelu_slope(hidden_two)).astype(jnp.bfloat16)
    second_part = filter_grad(padded_act, delta_two, rows, cols)
    act_grad = conv_taps(extend(delta_two), second_filter, rows, cols, True)
    delta_one = (act_grad * gelu_slope(hidden_one)).astype(jnp.bfloat16)
    first_part = filter_grad(padded_in, delta_one, rows, cols)
    first_grad, second_grad = lax.psum((first_part, second_part), ("lat", "lon"))
    input_grad = conv_taps(extend(delta_one), first_filter, rows, cols, True).astype(jnp.bfloat16)
    return (input_grad, first_grad, second_grad)


def solution(mesh):
    in_specs = (P("lat", "lon", None), P(), P(), P("lat", "lon", None))
    out_specs = (P("lat", "lon", None), P(), P())
    return jax.shard_map(body, mesh=mesh, in_specs=in_specs, out_specs=out_specs, check_vma=False)
```

profile of v0, /device:TPU:0, one launch (start us, length us, event | category | flops | bytes accessed | tf_op | source)
XLA Modules:
  0.0 228.8 jit_solution(7460417335077282387)
XLA Ops:
  7.2 0.8 fusion.133
  8.6 2.9 %collective-permute-start.1 = (bf16[1,96,256]{2,1,0:T(8,128)(2,1)S(1)}, bf16[1,96,256]{2,1,0:T(8,128)(2,1)S(1)}, u32[]{:S(2)}, u32[]{:S(2)}) collective-permute-start(bf16[1,96,256]{2,1,0:T(8,128)(2,1)S(1)} %get-tuple-element.55), channel_id=1, source_target_pairs={{4,0},{8,4},{12,8},{16,12},{20,16},{24,20},{28,24},{0,28},{5,1},{9... | collective-permute-start | bytes 147464 | tf_op jit(solution)/shard_map/ppermute | solution.py:16
  11.5 1.7 collective-permute-done
  13.2 1.2 constant_dynamic-update-slice_fusion.1
  14.5 4.4 %collective-permute-start.3 = (bf16[18,1,256]{2,1,0:T(2,128)(2,1)S(1)}, bf16[18,1,256]{2,1,0:T(2,128)(2,1)S(1)}, u32[]{:S(2)}, u32[]{:S(2)}) collective-permute-start(bf16[18,1,256]{2,1,0:T(2,128)(2,1)S(1)} %get-tuple-element.48), channel_id=1, source_target_pairs={{1,0},{2,1},{3,2},{0,3},{5,4},{6,5},{7,6},{4,7},{9,8},{10,9},{11,1... | collective-permute-start | bytes 27656 | tf_op jit(solution)/shard_map/ppermute | solution.py:16
  18.9 1.5 collective-permute-done.3
  20.3 4.1 %collective-permute-done.2 = bf16[18,1,256]{2,1,0:T(2,128)(2,1)S(1)} collective-permute-done((bf16[18,1,256]{2,1,0:T(2,128)(2,1)S(1)}, bf16[18,1,256]{2,1,0:T(2,128)(2,1)S(1)}, u32[]{:S(2)}, u32[]{:S(2)}) %collective-permute-start.2) | collective-permute-done | bytes 9248 | tf_op jit(solution)/shard_map/ppermute | solution.py:13
  25.0 0.8 fusion.128
  30.5 1.4 collective-permute-done.5
  31.9 2.6 %collective-permute-done.4 = bf16[1,96,256]{2,1,0:T(8,128)(2,1)S(1)} collective-permute-done((bf16[1,96,256]{2,1,0:T(8,128)(2,1)S(1)}, bf16[1,96,256]{2,1,0:T(8,128)(2,1)S(1)}, u32[]{:S(2)}, u32[]{:S(2)}) %collective-permute-start.4) | collective-permute-done | bytes 49184 | tf_op jit(solution)/shard_map/ppermute | solution.py:13
  34.8 1.8 collective-permute-start.6
  36.6 1.7 collective-permute-done.7
  38.4 2.0 collective-permute-done.6
  40.9 1.1 fusion.127
  45.5 0.7 copy-done.5
  46.3 0.7 fusion.6
  51.0 1.1 collective-permute-done.8
  52.2 2.0 collective-permute-start.10
  54.7 1.3 collective-permute-done.11
  56.0 1.9 collective-permute-done.10
  58.4 1.1 fusion.126
  63.1 0.7 fusion.12
  64.2 0.6 collective-permute-start.13
  67.8 1.4 collective-permute-done.12
  69.3 2.0 collective-permute-start.14
  71.8 1.4 copy-done.4
  73.2 2.0 collective-permute-done.14
  75.7 1.1 fusion.125
  80.1 1.3 fusion
  81.4 135.8 %all-reduce.3.cloned.1.call-done = (f32[3,3,256,256]{3,2,1,0:T(8,128)}, f32[3,3,256,256]{3,2,1,0:T(8,128)}) async-done(((f32[3,3,256,256]{3,2,1,0:T(8,128)}, f32[3,3,256,256]{3,2,1,0:T(8,128)}), (f32[3,3,256,256]{3,2,1,0:T(8,128)}, f32[3,3,256,256]{3,2,1,0:T(8,128)})) %all-reduce.3.cloned.1.call-update) | async-done | bytes 4718608 | tf_op jit(solution)/shard_map/psum | solution.py:93
  217.2 3.4 %copy.27 = f32[3,3,256,256]{3,2,1,0:T(8,128)} copy(f32[3,3,256,256]{3,2,1,0:T(8,128)} %get-tuple-element.58) | data formatting | bytes 4718592
  220.5 1.4 copy.28
  (94 shorter events, 26.5 us)
Async XLA Ops:
  7.2 210.0 %all-reduce.3.cloned.1.call-start = ((), (), s32[]{:S(2)}) async-start(), calls=%async_computation | async-start | bytes 9437184 | tf_op jit(solution)/shard_map/psum | solution.py:93
  8.0 5.2 %collective-permute-start = (bf16[1,96,256]{2,1,0:T(8,128)(2,1)S(1)}, bf16[1,96,256]{2,1,0:T(8,128)(2,1)S(1)}, u32[]{:S(2)}, u32[]{:S(2)}) collective-permute-start(bf16[1,96,256]{2,1,0:T(8,128)(2,1)S(1)} %get-tuple-element.56), channel_id=1, source_target_pairs={{0,4},{4,8},{8,12},{12,16},{16,20},{20,24},{24,28},{28,0},{1,5},{5... | collective-permute-start | bytes 147464 | tf_op jit(solution)/shard_map/ppermute | solution.py:13
  8.6 5.8 %collective-permute-start.1 = (bf16[1,96,256]{2,1,0:T(8,128)(2,1)S(1)}, bf16[1,96,256]{2,1,0:T(8,128)(2,1)S(1)}, u32[]{:S(2)}, u32[]{:S(2)}) collective-permute-start(bf16[1,96,256]{2,1,0:T(8,128)(2,1)S(1)} %get-tuple-element.55), channel_id=1, source_target_pairs={{4,0},{8,4},{12,8},{16,12},{20,16},{24,20},{28,24},{0,28},{5,1},{9... | collective-permute-start | bytes 147464 | tf_op jit(solution)/shard_map/ppermute | solution.py:16
  14.5 5.9 %collective-permute-start.3 = (bf16[18,1,256]{2,1,0:T(2,128)(2,1)S(1)}, bf16[18,1,256]{2,1,0:T(2,128)(2,1)S(1)}, u32[]{:S(2)}, u32[]{:S(2)}) collective-permute-start(bf16[18,1,256]{2,1,0:T(2,128)(2,1)S(1)} %get-tuple-element.48), channel_id=1, source_target_pairs={{1,0},{2,1},{3,2},{0,3},{5,4},{6,5},{7,6},{4,7},{9,8},{10,9},{11,1... | collective-permute-start | bytes 27656 | tf_op jit(solution)/shard_map/ppermute | solution.py:16
  18.9 5.6 %collective-permute-start.2 = (bf16[18,1,256]{2,1,0:T(2,128)(2,1)S(1)}, bf16[18,1,256]{2,1,0:T(2,128)(2,1)S(1)}, u32[]{:S(2)}, u32[]{:S(2)}) collective-permute-start(bf16[18,1,256]{2,1,0:T(2,128)(2,1)S(1)} %get-tuple-element.47), channel_id=1, source_target_pairs={{0,1},{1,2},{2,3},{3,0},{4,5},{5,6},{6,7},{7,4},{8,9},{9,10},{10,1... | collective-permute-start | bytes 27656 | tf_op jit(solution)/shard_map/ppermute | solution.py:13
  25.0 1.3 copy-start.1
  30.0 2.0 collective-permute-start.5
  30.0 4.5 %collective-permute-start.4 = (bf16[1,96,256]{2,1,0:T(8,128)(2,1)S(1)}, bf16[1,96,256]{2,1,0:T(8,128)(2,1)S(1)}, u32[]{:S(2)}, u32[]{:S(2)}) collective-permute-start(bf16[1,96,256]{2,1,0:T(8,128)(2,1)S(1)} %get-tuple-element.53), channel_id=1, source_target_pairs={{0,4},{4,8},{8,12},{12,16},{16,20},{20,24},{24,28},{28,0},{1,5},{5... | collective-permute-start | bytes 147464 | tf_op jit(solution)/shard_map/ppermute | solution.py:13
  34.5 3.8 %collective-permute-start.7 = (bf16[18,1,256]{2,1,0:T(2,128)(2,1)S(1)}, bf16[18,1,256]{2,1,0:T(2,128)(2,1)S(1)}, u32[]{:S(2)}, u32[]{:S(2)}) collective-permute-start(bf16[18,1,256]{2,1,0:T(2,128)(2,1)S(1)} %get-tuple-element.46), channel_id=1, source_target_pairs={{1,0},{2,1},{3,2},{0,3},{5,4},{6,5},{7,6},{4,7},{9,8},{10,9},{11,1... | collective-permute-start | bytes 27656 | tf_op jit(solution)/shard_map/ppermute | solution.py:16
  34.8 5.6 %collective-permute-start.6 = (bf16[18,1,256]{2,1,0:T(2,128)(2,1)S(1)}, bf16[18,1,256]{2,1,0:T(2,128)(2,1)S(1)}, u32[]{:S(2)}, u32[]{:S(2)}) collective-permute-start(bf16[18,1,256]{2,1,0:T(2,128)(2,1)S(1)} %get-tuple-element.45), channel_id=1, source_target_pairs={{0,1},{1,2},{2,3},{3,0},{4,5},{5,6},{6,7},{7,4},{8,9},{9,10},{10,1... | collective-permute-start | bytes 27656 | tf_op jit(solution)/shard_map/ppermute | solution.py:13
  40.9 1.3 copy-start
  45.1 1.1 copy-start.5
  47.4 3.6 %collective-permute-start.9 = (bf16[1,96,256]{2,1,0:T(8,128)(2,1)S(1)}, bf16[1,96,256]{2,1,0:T(8,128)(2,1)S(1)}, u32[]{:S(2)}, u32[]{:S(2)}) collective-permute-start(bf16[1,96,256]{2,1,0:T(8,128)(2,1)S(1)} %get-tuple-element.52), channel_id=1, source_target_pairs={{4,0},{8,4},{12,8},{16,12},{20,16},{24,20},{28,24},{0,28},{5,1},{9... | collective-permute-start | bytes 147464 | tf_op jit(solution)/shard_map/ppermute | solution.py:16
  47.5 4.6 %collective-permute-start.8 = (bf16[1,96,256]{2,1,0:T(8,128)(2,1)S(1)}, bf16[1,96,256]{2,1,0:T(8,128)(2,1)S(1)}, u32[]{:S(2)}, u32[]{:S(2)}) collective-permute-start(bf16[1,96,256]{2,1,0:T(8,128)(2,1)S(1)} %get-tuple-element.51), channel_id=1, source_target_pairs={{0,4},{4,8},{8,12},{12,16},{16,20},{20,24},{24,28},{28,0},{1,5},{5... | collective-permute-start | bytes 147464 | tf_op jit(solution)/shard_map/ppermute | solution.py:13
  52.2 3.8 %collective-permute-start.11 = (bf16[18,1,256]{2,1,0:T(2,128)(2,1)S(1)}, bf16[18,1,256]{2,1,0:T(2,128)(2,1)S(1)}, u32[]{:S(2)}, u32[]{:S(2)}) collective-permute-start(bf16[18,1,256]{2,1,0:T(2,128)(2,1)S(1)} %get-tuple-element.44), channel_id=1, source_target_pairs={{1,0},{2,1},{3,2},{0,3},{5,4},{6,5},{7,6},{4,7},{9,8},{10,9},{11,1... | collective-permute-start | bytes 27656 | tf_op jit(solution)/shard_map/ppermute | solution.py:16
  52.2 5.6 %collective-permute-start.10 = (bf16[18,1,256]{2,1,0:T(2,128)(2,1)S(1)}, bf16[18,1,256]{2,1,0:T(2,128)(2,1)S(1)}, u32[]{:S(2)}, u32[]{:S(2)}) collective-permute-start(bf16[18,1,256]{2,1,0:T(2,128)(2,1)S(1)} %get-tuple-element.43), channel_id=1, source_target_pairs={{0,1},{1,2},{2,3},{3,0},{4,5},{5,6},{6,7},{7,4},{8,9},{9,10},{10,1... | collective-permute-start | bytes 27656 | tf_op jit(solution)/shard_map/ppermute | solution.py:13
  54.7 4.8 %copy-start.3 = (f32[9,256,256]{2,1,0:T(8,128)}, f32[9,256,256]{2,1,0:T(8,128)S(1)}, u32[]{:S(2)}) copy-start(f32[9,256,256]{2,1,0:T(8,128)S(1)} %fusion.13) | copy-start | bytes 7077892
  64.2 3.6 %collective-permute-start.13 = (bf16[1,96,256]{2,1,0:T(8,128)(2,1)S(1)}, bf16[1,96,256]{2,1,0:T(8,128)(2,1)S(1)}, u32[]{:S(2)}, u32[]{:S(2)}) collective-permute-start(bf16[1,96,256]{2,1,0:T(8,128)(2,1)S(1)} %get-tuple-element.50), channel_id=1, source_target_pairs={{4,0},{8,4},{12,8},{16,12},{20,16},{24,20},{28,24},{0,28},{5,1},{9... | collective-permute-start | bytes 147464 | tf_op jit(solution)/shard_map/ppermute | solution.py:16
  64.8 4.4 %collective-permute-start.12 = (bf16[1,96,256]{2,1,0:T(8,128)(2,1)S(1)}, bf16[1,96,256]{2,1,0:T(8,128)(2,1)S(1)}, u32[]{:S(2)}, u32[]{:S(2)}) collective-permute-start(bf16[1,96,256]{2,1,0:T(8,128)(2,1)S(1)} %get-tuple-element.49), channel_id=1, source_target_pairs={{0,4},{4,8},{8,12},{12,16},{16,20},{20,24},{24,28},{28,0},{1,5},{5... | collective-permute-start | bytes 147464 | tf_op jit(solution)/shard_map/ppermute | solution.py:13
  69.2 3.9 %collective-permute-start.15 = (bf16[18,1,256]{2,1,0:T(2,128)(2,1)S(1)}, bf16[18,1,256]{2,1,0:T(2,128)(2,1)S(1)}, u32[]{:S(2)}, u32[]{:S(2)}) collective-permute-start(bf16[18,1,256]{2,1,0:T(2,128)(2,1)S(1)} %get-tuple-element.42), channel_id=1, source_target_pairs={{1,0},{2,1},{3,2},{0,3},{5,4},{6,5},{7,6},{4,7},{9,8},{10,9},{11,1... | collective-permute-start | bytes 27656 | tf_op jit(solution)/shard_map/ppermute | solution.py:16
  69.3 5.8 %collective-permute-start.14 = (bf16[18,1,256]{2,1,0:T(2,128)(2,1)S(1)}, bf16[18,1,256]{2,1,0:T(2,128)(2,1)S(1)}, u32[]{:S(2)}, u32[]{:S(2)}) collective-permute-start(bf16[18,1,256]{2,1,0:T(2,128)(2,1)S(1)} %get-tuple-element.41), channel_id=1, source_target_pairs={{0,1},{1,2},{2,3},{3,0},{4,5},{5,6},{6,7},{7,4},{8,9},{9,10},{10,1... | collective-permute-start | bytes 27656 | tf_op jit(solution)/shard_map/ppermute | solution.py:13
  71.7 1.4 copy-start.4
  217.2 3.4 %copy-start.2 = (f32[3,3,256,256]{3,2,1,0:T(8,128)S(1)}, f32[3,3,256,256]{3,2,1,0:T(8,128)}, u32[]{:S(2)}) copy-start(f32[3,3,256,256]{3,2,1,0:T(8,128)} %get-tuple-element.59) | copy-start | bytes 7077892
Sparse Core Ops, SparseCore 0:
  73.3 143.8 all-reduce.2
where the time goes:
time: 229 us
  waiting for transfers between devices  158 us (69%)
  matrix products  22.3 us (10%)
  starting transfers between devices  15.8 us (7%)
  between operations  14.6 us (6%)
  local copies, waits for them, and re-layouts  13.6 us (6%)
  other arithmetic  4.03 us (2%)
    psum x1, waiting for transfers between devices, body(): lax.psum((first_part, second_part), ('lat', 'lon'))  136 us
    ppermute x8, waiting for transfers between devices, extended(): lax.ppermute(lax.slice_in_dim(block, block.shape[dim] - width, None, axis...  16.7 us
    unnamed x16, local copies, waits for them, and re-layouts  8.77 us
    ppermute x8, starting transfers between devices, extended(): lax.ppermute(lax.slice_in_dim(block, 0, width, axis=dim), axis, backward)  8.4 us
    dot_general x18, matrix products, conv_taps(): lax.dot_general(piece, weight[2 - first, 2 - second], (((1,), (1,)), ((),...  8.18 us
    dot_general x18, matrix products, filter_grad(): lax.dot_general(piece, flat, (((0,), (0,)), ((), ())), preferred_element_...  7.54 us
    ppermute x8, starting transfers between devices, extended(): lax.ppermute(lax.slice_in_dim(block, block.shape[dim] - width, None, axis...  7.38 us
    dot_general x18, matrix products, conv_taps(): jnp.dot(piece, weight[first, second], preferred_element_type=jnp.float32)  6.59 us
  transfers between devices with their start and end apart: 17, of which 13 were waited for; matrix products, arithmetic and copies ran while one was open for 6% of the time, Pallas kernels for 0%

commit v1 on v0

v1 whole, which is shorter than its diff:
```python
import functools

import jax
import jax.numpy as jnp
from jax import lax
from jax.experimental import pallas as pl
from jax.experimental.pallas import tpu as pltpu
from jax.sharding import PartitionSpec as P

F32 = jnp.float32
BF16 = jnp.bfloat16
AXES = ("lat", "lon")
TAIL = 16
ROWS_PER_DOT = 2


def gelu_parts(h):
    cdf = 0.5 * (1.0 + lax.erf(h * 0.7071067811865476))
    slope = cdf + h * jnp.exp(-0.5 * h * h) * 0.3989422804014327
    return h * cdf, slope


def put(ref, row, pitch, value):
    at = pl.ds(row * pitch, pitch)
    ref[0, at, :] = pltpu.roll(value, 1, 0).astype(BF16)
    ref[1, at, :] = value.astype(BF16)
    ref[2, at, :] = pltpu.roll(value, pitch - 1, 0).astype(BF16)


def conv(source, weight, first, rows, pitch, flipped):
    total = None
    for a in range(3):
        for b in range(3):
            row = first + (2 - a if flipped else a)
            shift = 2 - b if flipped else b
            part = jnp.dot(
                source[shift, pl.ds(row * pitch, rows * pitch), :],
                weight[a, b],
                preferred_element_type=F32,
            )
            total = part if total is None else total + part
    return total


def filter_grad(source, first, delta, delta_first, rows, cols, pitch, out):
    flat = jnp.concatenate(
        [delta[1, pl.ds((delta_first + i) * pitch, cols), :] for i in range(rows)], axis=0
    ).T
    for a in range(3):
        for b in range(3):
            cells = jnp.concatenate(
                [source[b, pl.ds((first + a + i) * pitch, cols), :] for i in range(rows)], axis=0
            )
            part = jnp.dot(flat, cells, preferred_element_type=F32)
            out[a, b] = part.T.astype(out.dtype)


def spans(rows):
    return [(s, min(ROWS_PER_DOT, rows - s)) for s in range(0, rows, ROWS_PER_DOT)]


def kernel(
    R, C, edge, x, c, low, high, tail, w1, w2, w1t, w2t,
    input_grad, first_grad, second_grad, xs, acts, slopes, d2, d1,
):
    pitch = C + TAIL
    ch = x.shape[-1]
    for r in range(R + 8):
        own = low[r] if r < 4 else x[r - 4] if r < R + 4 else high[r - R - 4]
        put(xs, r, pitch, jnp.concatenate([own.astype(F32), tail[r].astype(F32)], axis=0))
    for s, n in spans(R + 6):
        h = conv(xs, w1, s, n, pitch, False)
        for k in range(n):
            value, slope = gelu_parts(h[k * pitch : (k + 1) * pitch])
            put(acts, s + k, pitch, value)
            slopes[pl.ds((s + k) * pitch, pitch), :] = slope
    for side, start in ((0, 0), (1, R + 3)):

        @pl.when(edge[side] == 1)
        def _():
            at = pl.ds(start * pitch, 3 * pitch)
            for b in range(3):
                acts[b, at, :] = jnp.zeros((3 * pitch, ch), BF16)
            slopes[at, :] = jnp.zeros((3 * pitch, ch), F32)

    for s, n in spans(R + 4):
        h = conv(acts, w2, s, n, pitch, False)
        for k in range(n):
            r = s + k
            own = low[r + 4] if r < 2 else c[r - 2] if r < R + 2 else high[r - R + 2]
            cot = jnp.concatenate([own.astype(F32), tail[R + 8 + r].astype(F32)], axis=0)
            put(d2, r, pitch, cot * gelu_parts(h[k * pitch : (k + 1) * pitch])[1])
    filter_grad(acts, 2, d2, 2, R, C, pitch, second_grad)
    for s, n in spans(R + 2):
        h = conv(d2, w2t, s, n, pitch, True)
        for k in range(n):
            at = pl.ds((s + k + 2) * pitch, pitch)
            put(d1, s + k, pitch, h[k * pitch : (k + 1) * pitch] * slopes[at, :])
    filter_grad(xs, 3, d1, 1, R, C, pitch, first_grad)
    for s, n in spans(R):
        h = conv(d1, w1t, s, n, pitch, True)
        for k in range(n):
            input_grad[s + k] = h[k * pitch : k * pitch + C].astype(BF16)


def block_step(edge, x, c, low, high, tail, w1, w2):
    R, C, ch = x.shape
    pitch = C + TAIL
    vmem = pl.BlockSpec(memory_space=pltpu.VMEM)
    filters = jax.ShapeDtypeStruct(w1.shape, BF16)
    return pl.pallas_call(
        functools.partial(kernel, R, C),
        out_shape=[jax.ShapeDtypeStruct(x.shape, BF16), filters, filters],
        in_specs=[pl.BlockSpec(memory_space=pltpu.SMEM)] + [vmem] * 9,
        out_specs=[vmem] * 3,
        scratch_shapes=[
            pltpu.VMEM((3, (R + 8) * pitch, ch), BF16),
            pltpu.VMEM((3, (R + 6) * pitch, ch), BF16),
            pltpu.VMEM(((R + 6) * pitch, ch), F32),
            pltpu.VMEM((3, (R + 4) * pitch, ch), BF16),
            pltpu.VMEM((3, (R + 2) * pitch, ch), BF16),
        ],
        compiler_params=pltpu.CompilerParams(vmem_limit_bytes=40 * 2**20),
    )(edge, x, c, low, high, tail, w1, w2, jnp.swapaxes(w1, 2, 3), jnp.swapaxes(w2, 2, 3))


def halos(x, c):
    R, C, ch = x.shape
    L, Z = lax.axis_size("lat"), lax.axis_size("lon")
    up = [(i, i + 1) for i in range(L - 1)]
    down = [(i + 1, i) for i in range(L - 1)]
    low = lax.ppermute(jnp.concatenate([x[R - 4 :], c[R - 2 :]], axis=0), "lat", up)
    high = lax.ppermute(jnp.concatenate([x[:4], c[:2]], axis=0), "lat", down)

    def columns(start):
        parts = [low[:4], x, high[:4], low[4:], c, high[4:]]
        taken = jnp.concatenate([p[:, start : start + 4] for p in parts], axis=0)
        return taken.reshape(-1, 8, ch)

    east = [(i, (i + 1) % Z) for i in range(Z)]
    west = [(d, s) for s, d in east]
    left = lax.ppermute(columns(C - 4), "lon", east).reshape(-1, 4, ch)
    right = lax.ppermute(columns(0), "lon", west).reshape(-1, 4, ch)
    gap = jnp.zeros((left.shape[0], TAIL - 8, ch), BF16)
    return low, high, jnp.concatenate([right, gap, left], axis=1)


def total(part):
    L, Z = lax.axis_size("lat"), lax.axis_size("lon")
    N = L * Z
    lat = [Z << k for k in range(L.bit_length() - 1)]
    lon = [1 << k for k in range(Z.bit_length() - 1)]
    core, rest = lat[0], lat[1:]
    steps = [(core, core)] + list(zip(rest + lon, rest[::-1] + lon))
    me = lax.axis_index("lat") * Z + lax.axis_index("lon")
    halved = steps[: len(steps) - min(2, len(lon))]

    def exchange(v, bits):
        pairs = [(i, i ^ bits[1 if i & core else 0]) for i in range(N)]
        return lax.ppermute(v, AXES, pairs)

    def side(bits):
        return (me // jnp.where(me & core == 0, bits[0], bits[1])) % 2

    v = part
    for bits in halved:
        half = v.shape[0] // 2
        give = lax.dynamic_slice_in_dim(v, (1 - side(bits)) * half, half).astype(BF16)
        keep = lax.dynamic_slice_in_dim(v, side(bits) * half, half).astype(F32)
        v = keep + exchange(give, bits).astype(F32)
    for bits in steps[len(halved) :]:
        v = v.astype(BF16)
        v = v.astype(F32) + exchange(v, bits).astype(F32)
    v = v.astype(BF16)
    for bits in halved[::-1]:
        other = exchange(v, bits)
        v = jnp.where(
            side(bits) == 0, jnp.concatenate([v, other]), jnp.concatenate([other, v])
        )
    return v.astype(F32)


def body(inputs, first_filter, second_filter, cotangent):
    index, count = lax.axis_index("lat"), lax.axis_size("lat")
    edge = jnp.stack([index == 0, index == count - 1]).astype(jnp.int32)
    low, high, tail = halos(inputs, cotangent)
    input_grad, first_part, second_part = block_step(
        edge, inputs, cotangent, low, high, tail, first_filter, second_filter
    )
    ch = inputs.shape[-1]
    second_grad = total(second_part.reshape(-1, ch)).reshape(second_filter.shape)
    first_grad = total(first_part.reshape(-1, ch)).reshape(first_filter.shape)
    return input_grad, first_grad, second_grad


def solution(mesh):
    in_specs = (P("lat", "lon", None), P(), P(), P("lat", "lon", None))
    out_specs = (P("lat", "lon", None), P(), P())
    return jax.shard_map(body, mesh=mesh, in_specs=in_specs, out_specs=out_specs, check_vma=False)
```

time: 229 us -> 118 us (0.52)
  waiting for transfers between devices: 158 us -> 38.4 us
  matrix products: 22.3 us -> 0 us
  Pallas kernels: 0 us -> 17.9 us
  between operations: 14.6 us -> 0.91 us
  local copies, waits for them, and re-layouts: 13.6 us -> 25.3 us
  starting transfers between devices: 15.8 us -> 26.9 us
  other arithmetic: 4.03 us -> 7.84 us
    psum x1 -> x0, waiting for transfers between devices: 136 us -> none  [body(): lax.psum((first_part, second_part), ('lat', 'lon'))]
    dot_general x54 -> x0, matrix products: 22.3 us -> none  [the longest x18 8.18 us: conv_taps(): lax.dot_general(piece, weight[2 - first, 2 - second], (((1,), (1,)), ((),...]
    pallas_call x0 -> x1, Pallas kernels: none -> 17.9 us  [block_step(): pl.pallas_call(functools.partial(kernel, R, C), out_shape=[jax.ShapeDtype...]
    ppermute x16 -> x20, waiting for transfers between devices: 22.6 us -> 38.4 us  [the longest x16 34.4 us: exchange(): return lax.ppermute(v, AXES, pairs)]
    ppermute x16 -> x20, starting transfers between devices: 15.8 us -> 26.9 us  [the longest x16 18.1 us: exchange(): return lax.ppermute(v, AXES, pairs)]
    unnamed x16 -> x25, local copies, waits for them, and re-layouts: 8.77 us -> 15.4 us
    reshape x0 -> x4, local copies, waits for them, and re-layouts: none -> 6.22 us  [the longest x2 3.11 us: columns(): return taken.reshape(-1, 8, ch)]
    slice x9 -> x2, local copies, waits for them, and re-layouts: 4.87 us -> 2.1 us  [halos(): high = lax.ppermute(jnp.concatenate([x[:4], c[:2]], axis=0), 'lat', down)]
  transfers between devices with their start and end apart: 17 -> 20, of which waited for: 13 -> 14; matrix products, arithmetic and copies ran while one was open for 6% -> 9% of each run, Pallas kernels for 0% -> 0%
where the time goes in v1:
time: 118 us; the launch traced here: 117 us
  waiting for transfers between devices  38.4 us (33%)
  starting transfers between devices  26.9 us (23%)
  local copies, waits for them, and re-layouts  25.3 us (21%)
  Pallas kernels  17.9 us (15%)
  other arithmetic  7.84 us (7%)
    ppermute x16, waiting for transfers between devices, exchange(): return lax.ppermute(v, AXES, pairs)  34.4 us
    ppermute x16, starting transfers between devices, exchange(): return lax.ppermute(v, AXES, pairs)  18.1 us
    pallas_call x1, Pallas kernels, block_step(): pl.pallas_call(functools.partial(kernel, R, C), out_shape=[jax.ShapeDtype...  17.9 us
    unnamed x25, local copies, waits for them, and re-layouts  15.4 us
    convert_element_type x2, other arithmetic, total(): return v.astype(F32)  3.26 us
    reshape x2, local copies, waits for them, and re-layouts, columns(): return taken.reshape(-1, 8, ch)  3.11 us
    ppermute x1, starting transfers between devices, halos(): lax.ppermute(jnp.concatenate([x[R - 4:], c[R - 2:]], axis=0), 'lat', up)  3.1 us
    ppermute x1, waiting for transfers between devices, halos(): left = lax.ppermute(columns(C - 4), 'lon', east).reshape(-1, 4, ch)  2.85 us
  transfers between devices with their start and end apart: 20, of which 14 were waited for; matrix products, arithmetic and copies ran while one was open for 9% of the time, Pallas kernels for 0%

profile of v1, /device:TPU:0, one launch (start us, length us, event | category | flops | bytes accessed | tf_op | source)
XLA Modules:
  0.0 117.2 jit_solution(6685736490884815118)
XLA Ops:
  3.5 3.1 %collective-permute-start = (bf16[6,96,256]{2,1,0:T(8,128)(2,1)}, bf16[6,96,256]{2,1,0:T(8,128)(2,1)}, u32[]{:S(2)}, u32[]{:S(2)}) collective-permute-start(bf16[6,96,256]{2,1,0:T(8,128)(2,1)} %pad_maximum_fusion.1), channel_id=1, source_target_pairs={{0,4},{4,8},{8,12},{12,16},{16,20},{20,24},{24,28},{1,5},{5,9},{9,... | collective-permute-start | bytes 884744 | tf_op jit(solution)/shard_map/ppermute | solution.py:132
  9.9 1.5 %copy.10 = bf16[3,3,256,256]{2,3,1,0:T(8,128)(2,1)} copy(bf16[3,3,256,256]{3,2,1,0:T(8,128)(2,1)S(1)} %copy-done.1) | data formatting | bytes 2359296 | tf_op args[2]
  11.6 1.3 %constant_dynamic-update-slice_fusion.3 = (bf16[44,4,256]{2,1,0:T(4,128)(2,1)}, bf16[44,4,256]{2,1,0:T(4,128)(2,1)}) fusion(bf16[6,96,256]{2,1,0:T(8,128)(2,1)} %collective-permute-done.low), kind=kLoop, calls=%fused_computation.30 | loop fusion | bytes 32768
  12.9 1.5 %slice_dynamic-update-slice_fusion.3 = (bf16[44,4,256]{2,1,0:T(4,128)(2,1)}, bf16[44,4,256]{2,1,0:T(4,128)(2,1)}) fusion(bf16[44,4,256]{2,1,0:T(4,128)(2,1)} %get-tuple-element.23, bf16[16,96,256]{2,1,0:T(8,128)(2,1)} %x.1, bf16[44,4,256]{2,1,0:T(4,128)(2,1)} %get-tuple-element.24), kind=kLoop, calls=%fused_computation.26 | loop fusion | bytes 131072
  14.4 1.3 %constant_dynamic-update-slice_fusion.2 = (bf16[44,4,256]{2,1,0:T(4,128)(2,1)}, bf16[44,4,256]{2,1,0:T(4,128)(2,1)}) fusion(bf16[44,4,256]{2,1,0:T(4,128)(2,1)} %get-tuple-element.11, bf16[6,96,256]{2,1,0:T(8,128)(2,1)} %collective-permute-done.1.high, bf16[44,4,256]{2,1,0:T(4,128)(2,1)} %get-tuple-element.12), kind=kLoop, calls=%fused_computation.29 | loop fusion | bytes 32768
  15.8 1.3 %constant_dynamic-update-slice_fusion.1 = (bf16[44,4,256]{2,1,0:T(4,128)(2,1)}, bf16[44,4,256]{2,1,0:T(4,128)(2,1)}) fusion(bf16[44,4,256]{2,1,0:T(4,128)(2,1)} %get-tuple-element.21, bf16[6,96,256]{2,1,0:T(8,128)(2,1)} %collective-permute-done.low, bf16[44,4,256]{2,1,0:T(4,128)(2,1)} %get-tuple-element.22), kind=kLoop, calls=%fused_computation.28 | loop fusion | bytes 16384
  17.1 1.5 %slice_dynamic-update-slice_fusion.2 = (bf16[44,4,256]{2,1,0:T(4,128)(2,1)}, bf16[44,4,256]{2,1,0:T(4,128)(2,1)}) fusion(bf16[44,4,256]{2,1,0:T(4,128)(2,1)} %get-tuple-element.19, bf16[16,96,256]{2,1,0:T(8,128)(2,1)} %c.1, bf16[44,4,256]{2,1,0:T(4,128)(2,1)} %get-tuple-element.20), kind=kLoop, calls=%fused_computation.25 | loop fusion | bytes 131072
  18.6 1.3 %constant_dynamic-update-slice_fusion = (bf16[44,4,256]{2,1,0:T(4,128)(2,1)}, bf16[44,4,256]{2,1,0:T(4,128)(2,1)}) fusion(bf16[44,4,256]{2,1,0:T(4,128)(2,1)} %get-tuple-element.9, bf16[6,96,256]{2,1,0:T(8,128)(2,1)} %collective-permute-done.1.high, bf16[44,4,256]{2,1,0:T(4,128)(2,1)} %get-tuple-element.10), kind=kLoop, calls=%fused_computation.27 | loop fusion | bytes 16384 | tf_op jit(solution)/shard_map/concatenate | solution.py:137
  19.9 1.6 %reshape.38 = bf16[22,8,256]{2,1,0:T(8,128)(2,1)} reshape(bf16[44,4,256]{2,1,0:T(4,128)(2,1)} %get-tuple-element.17) | data formatting | bytes 180224 | tf_op jit(solution)/shard_map/reshape | solution.py:138
  21.5 1.6 %reshape.40 = bf16[22,8,256]{2,1,0:T(8,128)(2,1)} reshape(bf16[44,4,256]{2,1,0:T(4,128)(2,1)} %get-tuple-element.18) | data formatting | bytes 180224 | tf_op jit(solution)/shard_map/reshape | solution.py:138
  23.0 2.4 %collective-permute-start.3 = (bf16[22,8,256]{2,1,0:T(8,128)(2,1)}, bf16[22,8,256]{2,1,0:T(8,128)(2,1)}, u32[]{:S(2)}, u32[]{:S(2)}) collective-permute-start(bf16[22,8,256]{2,1,0:T(8,128)(2,1)} %reshape.40), channel_id=1, source_target_pairs={{0,1},{1,2},{2,3},{3,0},{4,5},{5,6},{6,7},{7,4},{8,9},{9,10},{10,1... | collective-permute-start | bytes 270344 | tf_op jit(solution)/shard_map/ppermute | solution.py:142
  25.4 2.0 %collective-permute-start.2 = (bf16[22,8,256]{2,1,0:T(8,128)(2,1)}, bf16[22,8,256]{2,1,0:T(8,128)(2,1)}, u32[]{:S(2)}, u32[]{:S(2)}) collective-permute-start(bf16[22,8,256]{2,1,0:T(8,128)(2,1)} %reshape.38), channel_id=1, source_target_pairs={{1,0},{2,1},{3,2},{0,3},{5,4},{6,5},{7,6},{4,7},{9,8},{10,9},{11,1... | collective-permute-start | bytes 270344 | tf_op jit(solution)/shard_map/ppermute | solution.py:143
  27.5 2.8 %collective-permute-done.3 = bf16[22,8,256]{2,1,0:T(8,128)(2,1)} collective-permute-done((bf16[22,8,256]{2,1,0:T(8,128)(2,1)}, bf16[22,8,256]{2,1,0:T(8,128)(2,1)}, u32[]{:S(2)}, u32[]{:S(2)}) %collective-permute-start.3) | collective-permute-done | bytes 90144 | tf_op jit(solution)/shard_map/ppermute | solution.py:142
  30.4 1.6 %reshape.41 = bf16[44,4,256]{2,1,0:T(4,128)(2,1)} reshape(bf16[22,8,256]{2,1,0:T(8,128)(2,1)} %collective-permute-done.3) | data formatting | bytes 180224 | tf_op jit(solution)/shard_map/reshape | solution.py:142
  33.1 1.6 %reshape.39 = bf16[44,4,256]{2,1,0:T(4,128)(2,1)} reshape(bf16[22,8,256]{2,1,0:T(8,128)(2,1)} %collective-permute-done.2) | data formatting | bytes 180224 | tf_op jit(solution)/shard_map/reshape | solution.py:143
  39.3 17.9 %shard_map.67 = (bf16[16,96,256]{2,1,0:T(8,128)(2,1)}, bf16[3,3,256,256]{3,2,1,0:T(8,128)(2,1)S(1)}, bf16[3,3,256,256]{3,2,1,0:T(8,128)(2,1)S(1)}) custom-call(s32[2]{0:T(128)S(1)} %add_convert_fusion.6.edge, bf16[16,96,256]{2,1,0:T(8,128)(2,1)S(1)} %copy-done.3, bf16[16,96,256]{2,1,0:T(8,128)(2,1)S(1)} %copy-done.4, ...), custom_call_target="tpu_custom_call" | custom-call | tf_op jit(solution)/shard_map/pallas_call | solution.py:111
  61.9 2.9 %collective-permute-start.5 = (bf16[576,256]{1,0:T(8,128)(2,1)S(1)}, bf16[576,256]{1,0:T(8,128)(2,1)S(1)}, u32[]{:S(2)}, u32[]{:S(2)}) collective-permute-start(bf16[576,256]{1,0:T(8,128)(2,1)S(1)} %dynamic-slice_convert_fusion.1), channel_id=1, source_target_pairs={{0,8},{1,9},{2,10},{3,11},{4,20},{5,21},{6,22},{7,23},{8,0},{9,1},... | collective-permute-start | bytes 884744 | tf_op jit(solution)/shard_map/ppermute | solution.py:160
  65.0 4.6 %collective-permute-done.5 = bf16[576,256]{1,0:T(8,128)(2,1)S(1)} collective-permute-done((bf16[576,256]{1,0:T(8,128)(2,1)S(1)}, bf16[576,256]{1,0:T(8,128)(2,1)S(1)}, u32[]{:S(2)}, u32[]{:S(2)}) %collective-permute-start.5) | collective-permute-done | bytes 294944 | tf_op jit(solution)/shard_map/ppermute | solution.py:160
  69.7 2.9 %collective-permute-start.6 = (bf16[288,256]{1,0:T(8,128)(2,1)S(1)}, bf16[288,256]{1,0:T(8,128)(2,1)S(1)}, u32[]{:S(2)}, u32[]{:S(2)}) collective-permute-start(bf16[288,256]{1,0:T(8,128)(2,1)S(1)} %dynamic-slice_convert_fusion.3), channel_id=1, source_target_pairs={{0,16},{1,17},{2,18},{3,19},{4,12},{5,13},{6,14},{7,15},{8,24},{9,... | collective-permute-start | bytes 442376 | tf_op jit(solution)/shard_map/ppermute | solution.py:160
  73.4 3.8 %collective-permute-done.6 = bf16[288,256]{1,0:T(8,128)(2,1)S(1)} collective-permute-done((bf16[288,256]{1,0:T(8,128)(2,1)S(1)}, bf16[288,256]{1,0:T(8,128)(2,1)S(1)}, u32[]{:S(2)}, u32[]{:S(2)}) %collective-permute-start.6) | collective-permute-done | bytes 147488 | tf_op jit(solution)/shard_map/ppermute | solution.py:160
  77.3 2.0 %collective-permute-done.13 = bf16[576,256]{1,0:T(8,128)(2,1)S(1)} collective-permute-done((bf16[576,256]{1,0:T(8,128)(2,1)S(1)}, bf16[576,256]{1,0:T(8,128)(2,1)S(1)}, u32[]{:S(2)}, u32[]{:S(2)}) %collective-permute-start.13) | collective-permute-done | bytes 294944 | tf_op jit(solution)/shard_map/ppermute | solution.py:160
  79.5 2.9 %collective-permute-done.7 = bf16[288,256]{1,0:T(8,128)(2,1)S(1)} collective-permute-done((bf16[288,256]{1,0:T(8,128)(2,1)S(1)}, bf16[288,256]{1,0:T(8,128)(2,1)S(1)}, u32[]{:S(2)}, u32[]{:S(2)}) %collective-permute-start.7) | collective-permute-done | bytes 147488 | tf_op jit(solution)/shard_map/ppermute | solution.py:160
  82.5 1.4 %collective-permute-start.8 = (bf16[288,256]{1,0:T(8,128)(2,1)S(1)}, bf16[288,256]{1,0:T(8,128)(2,1)S(1)}, u32[]{:S(2)}, u32[]{:S(2)}) collective-permute-start(bf16[288,256]{1,0:T(8,128)(2,1)S(1)} %add_convert_fusion.4), channel_id=1, source_target_pairs={{0,2},{1,3},{2,0},{3,1},{4,6},{5,7},{6,4},{7,5},{8,10},{9,11},{10,... | collective-permute-start | bytes 442376 | tf_op jit(solution)/shard_map/ppermute | solution.py:160
  85.2 4.8 %collective-permute-done.8 = bf16[288,256]{1,0:T(8,128)(2,1)S(1)} collective-permute-done((bf16[288,256]{1,0:T(8,128)(2,1)S(1)}, bf16[288,256]{1,0:T(8,128)(2,1)S(1)}, u32[]{:S(2)}, u32[]{:S(2)}) %collective-permute-start.8) | collective-permute-done | bytes 147488 | tf_op jit(solution)/shard_map/ppermute | solution.py:160
  90.0 2.0 %collective-permute-start.9 = (bf16[288,256]{1,0:T(8,128)(2,1)S(1)}, bf16[288,256]{1,0:T(8,128)(2,1)S(1)}, u32[]{:S(2)}, u32[]{:S(2)}) collective-permute-start(bf16[288,256]{1,0:T(8,128)(2,1)S(1)} %add_convert_fusion.3), channel_id=1, source_target_pairs={{0,16},{1,17},{2,18},{3,19},{4,12},{5,13},{6,14},{7,15},{8,24},{9,... | collective-permute-start | bytes 442376 | tf_op jit(solution)/shard_map/ppermute | solution.py:160
  93.0 3.8 %collective-permute-done.9 = bf16[288,256]{1,0:T(8,128)(2,1)S(1)} collective-permute-done((bf16[288,256]{1,0:T(8,128)(2,1)S(1)}, bf16[288,256]{1,0:T(8,128)(2,1)S(1)}, u32[]{:S(2)}, u32[]{:S(2)}) %collective-permute-start.9) | collective-permute-done | bytes 147488 | tf_op jit(solution)/shard_map/ppermute | solution.py:160
  97.0 1.8 %collective-permute-start.10 = (bf16[576,256]{1,0:T(8,128)(2,1)S(1)}, bf16[576,256]{1,0:T(8,128)(2,1)S(1)}, u32[]{:S(2)}, u32[]{:S(2)}) collective-permute-start(bf16[576,256]{1,0:T(8,128)(2,1)S(1)} %maximum_select_fusion.4), channel_id=1, source_target_pairs={{0,8},{1,9},{2,10},{3,11},{4,20},{5,21},{6,22},{7,23},{8,0},{9,1},... | collective-permute-start | bytes 884744 | tf_op jit(solution)/shard_map/ppermute | solution.py:160
  99.8 1.8 %collective-permute-start.17 = (bf16[288,256]{1,0:T(8,128)(2,1)S(1)}, bf16[288,256]{1,0:T(8,128)(2,1)S(1)}, u32[]{:S(2)}, u32[]{:S(2)}) collective-permute-start(bf16[288,256]{1,0:T(8,128)(2,1)S(1)} %add_convert_fusion), channel_id=1, source_target_pairs={{0,16},{1,17},{2,18},{3,19},{4,12},{5,13},{6,14},{7,15},{8,24},{9,... | collective-permute-start | bytes 442376 | tf_op jit(solution)/shard_map/ppermute | solution.py:160
  101.6 4.5 %collective-permute-done.17 = bf16[288,256]{1,0:T(8,128)(2,1)S(1)} collective-permute-done((bf16[288,256]{1,0:T(8,128)(2,1)S(1)}, bf16[288,256]{1,0:T(8,128)(2,1)S(1)}, u32[]{:S(2)}, u32[]{:S(2)}) %collective-permute-start.17) | collective-permute-done | bytes 147488 | tf_op jit(solution)/shard_map/ppermute | solution.py:160
  107.8 5.2 %collective-permute-done.18 = bf16[576,256]{1,0:T(8,128)(2,1)S(1)} collective-permute-done((bf16[576,256]{1,0:T(8,128)(2,1)S(1)}, bf16[576,256]{1,0:T(8,128)(2,1)S(1)}, u32[]{:S(2)}, u32[]{:S(2)}) %collective-permute-start.18) | collective-permute-done | bytes 294944 | tf_op jit(solution)/shard_map/ppermute | solution.py:160
  113.7 1.6 %convert.2 = f32[3,3,256,256]{3,2,1,0:T(8,128)} convert(bf16[3,3,256,256]{3,2,1,0:T(8,128)(2,1)S(1)} %bitcast.17) | non-fusion elementwise | flops 589824 | bytes 3538944 | tf_op jit(solution)/shard_map/convert_element_type | solution.py:180
  115.6 1.6 %convert.3 = f32[3,3,256,256]{3,2,1,0:T(8,128)} convert(bf16[3,3,256,256]{3,2,1,0:T(8,128)(2,1)S(1)} %bitcast.16) | non-fusion elementwise | flops 589824 | bytes 3538944 | tf_op jit(solution)/shard_map/convert_element_type | solution.py:180
  (71 shorter events, 24.2 us)
Async XLA Ops:
  0.6 8.0 %copy-start = (bf16[3,3,256,256]{3,2,1,0:T(8,128)(2,1)S(1)}, bf16[3,3,256,256]{3,2,1,0:T(8,128)(2,1)}, u32[]{:S(2)}) copy-start(bf16[3,3,256,256]{3,2,1,0:T(8,128)(2,1)} %w1.1) | copy-start | bytes 3538948
  3.5 8.1 %collective-permute-start = (bf16[6,96,256]{2,1,0:T(8,128)(2,1)}, bf16[6,96,256]{2,1,0:T(8,128)(2,1)}, u32[]{:S(2)}, u32[]{:S(2)}) collective-permute-start(bf16[6,96,256]{2,1,0:T(8,128)(2,1)} %pad_maximum_fusion.1), channel_id=1, source_target_pairs={{0,4},{4,8},{8,12},{12,16},{16,20},{20,24},{24,28},{1,5},{5,9},{9,... | collective-permute-start | bytes 884744 | tf_op jit(solution)/shard_map/ppermute | solution.py:132
  7.3 7.1 %collective-permute-start.1 = (bf16[6,96,256]{2,1,0:T(8,128)(2,1)}, bf16[6,96,256]{2,1,0:T(8,128)(2,1)}, u32[]{:S(2)}, u32[]{:S(2)}) collective-permute-start(bf16[6,96,256]{2,1,0:T(8,128)(2,1)} %pad_maximum_fusion.2), channel_id=1, source_target_pairs={{4,0},{8,4},{12,8},{16,12},{20,16},{24,20},{28,24},{5,1},{9,5},{13... | collective-permute-start | bytes 884744 | tf_op jit(solution)/shard_map/ppermute | solution.py:133
  8.7 1.3 %copy-start.1 = (bf16[3,3,256,256]{3,2,1,0:T(8,128)(2,1)S(1)}, bf16[3,3,256,256]{3,2,1,0:T(8,128)(2,1)}, u32[]{:S(2)}) copy-start(bf16[3,3,256,256]{3,2,1,0:T(8,128)(2,1)} %w2.1) | copy-start | bytes 3538948
  23.0 7.3 %collective-permute-start.3 = (bf16[22,8,256]{2,1,0:T(8,128)(2,1)}, bf16[22,8,256]{2,1,0:T(8,128)(2,1)}, u32[]{:S(2)}, u32[]{:S(2)}) collective-permute-start(bf16[22,8,256]{2,1,0:T(8,128)(2,1)} %reshape.40), channel_id=1, source_target_pairs={{0,1},{1,2},{2,3},{3,0},{4,5},{5,6},{6,7},{7,4},{8,9},{9,10},{10,1... | collective-permute-start | bytes 270344 | tf_op jit(solution)/shard_map/ppermute | solution.py:142
  25.4 7.6 %collective-permute-start.2 = (bf16[22,8,256]{2,1,0:T(8,128)(2,1)}, bf16[22,8,256]{2,1,0:T(8,128)(2,1)}, u32[]{:S(2)}, u32[]{:S(2)}) collective-permute-start(bf16[22,8,256]{2,1,0:T(8,128)(2,1)} %reshape.38), channel_id=1, source_target_pairs={{1,0},{2,1},{3,2},{0,3},{5,4},{6,5},{7,6},{4,7},{9,8},{10,9},{11,1... | collective-permute-start | bytes 270344 | tf_op jit(solution)/shard_map/ppermute | solution.py:143
  35.8 1.3 %copy-start.2 = (bf16[3,3,256,256]{2,3,1,0:T(8,128)(2,1)S(1)}, bf16[3,3,256,256]{2,3,1,0:T(8,128)(2,1)}, u32[]{:S(2)}) copy-start(bf16[3,3,256,256]{2,3,1,0:T(8,128)(2,1)} %copy.10) | copy-start | bytes 3538948
  37.0 1.1 copy-start.3
  38.2 1.1 copy-start.4
  57.2 1.0 copy-start.5
  58.2 1.0 copy-start.7
  58.2 1.9 %copy-start.6 = (bf16[3,3,256,256]{3,2,1,0:T(8,128)(2,1)S(1)}, bf16[3,3,256,256]{3,2,1,0:T(8,128)(2,1)}, u32[]{:S(2)}) copy-start(bf16[3,3,256,256]{3,2,1,0:T(8,128)(2,1)} %copy-done.5) | copy-start | bytes 3538948
  59.3 2.5 %copy-start.8 = (bf16[3,3,256,256]{3,2,1,0:T(8,128)(2,1)S(1)}, bf16[3,3,256,256]{3,2,1,0:T(8,128)(2,1)}, u32[]{:S(2)}) copy-start(bf16[3,3,256,256]{3,2,1,0:T(8,128)(2,1)} %copy-done.7) | copy-start | bytes 3538948
  59.3 2.5 %collective-permute-start.4 = (bf16[1152,256]{1,0:T(8,128)(2,1)S(1)}, bf16[1152,256]{1,0:T(8,128)(2,1)S(1)}, u32[]{:S(2)}, u32[]{:S(2)}) collective-permute-start(bf16[1152,256]{1,0:T(8,128)(2,1)S(1)} %constant_dynamic-slice_fusion.1), channel_id=1, source_target_pairs={{0,4},{1,5},{2,6},{3,7},{4,0},{5,1},{6,2},{7,3},{8,12},{9,13},{10,... | collective-permute-start | bytes 1769480 | tf_op jit(solution)/shard_map/ppermute | solution.py:160
  60.1 4.7 %collective-permute-start.12 = (bf16[1152,256]{1,0:T(8,128)(2,1)S(1)}, bf16[1152,256]{1,0:T(8,128)(2,1)S(1)}, u32[]{:S(2)}, u32[]{:S(2)}) collective-permute-start(bf16[1152,256]{1,0:T(8,128)(2,1)S(1)} %constant_dynamic-slice_fusion), channel_id=1, source_target_pairs={{0,4},{1,5},{2,6},{3,7},{4,0},{5,1},{6,2},{7,3},{8,12},{9,13},{10,... | collective-permute-start | bytes 1769480 | tf_op jit(solution)/shard_map/ppermute | solution.py:160
  61.9 7.6 %collective-permute-start.5 = (bf16[576,256]{1,0:T(8,128)(2,1)S(1)}, bf16[576,256]{1,0:T(8,128)(2,1)S(1)}, u32[]{:S(2)}, u32[]{:S(2)}) collective-permute-start(bf16[576,256]{1,0:T(8,128)(2,1)S(1)} %dynamic-slice_convert_fusion.1), channel_id=1, source_target_pairs={{0,8},{1,9},{2,10},{3,11},{4,20},{5,21},{6,22},{7,23},{8,0},{9,1},... | collective-permute-start | bytes 884744 | tf_op jit(solution)/shard_map/ppermute | solution.py:160
  69.7 7.6 %collective-permute-start.6 = (bf16[288,256]{1,0:T(8,128)(2,1)S(1)}, bf16[288,256]{1,0:T(8,128)(2,1)S(1)}, u32[]{:S(2)}, u32[]{:S(2)}) collective-permute-start(bf16[288,256]{1,0:T(8,128)(2,1)S(1)} %dynamic-slice_convert_fusion.3), channel_id=1, source_target_pairs={{0,16},{1,17},{2,18},{3,19},{4,12},{5,13},{6,14},{7,15},{8,24},{9,... | collective-permute-start | bytes 442376 | tf_op jit(solution)/shard_map/ppermute | solution.py:160
  72.5 6.8 %collective-permute-start.13 = (bf16[576,256]{1,0:T(8,128)(2,1)S(1)}, bf16[576,256]{1,0:T(8,128)(2,1)S(1)}, u32[]{:S(2)}, u32[]{:S(2)}) collective-permute-start(bf16[576,256]{1,0:T(8,128)(2,1)S(1)} %dynamic-slice_convert_fusion), channel_id=1, source_target_pairs={{0,8},{1,9},{2,10},{3,11},{4,20},{5,21},{6,22},{7,23},{8,0},{9,1},... | collective-permute-start | bytes 884744 | tf_op jit(solution)/shard_map/ppermute | solution.py:160
  77.2 5.2 %collective-permute-start.7 = (bf16[288,256]{1,0:T(8,128)(2,1)S(1)}, bf16[288,256]{1,0:T(8,128)(2,1)S(1)}, u32[]{:S(2)}, u32[]{:S(2)}) collective-permute-start(bf16[288,256]{1,0:T(8,128)(2,1)S(1)} %add_convert_fusion.5), channel_id=1, source_target_pairs={{0,1},{1,0},{2,3},{3,2},{4,5},{5,4},{6,7},{7,6},{8,9},{9,8},{10,11... | collective-permute-start | bytes 442376 | tf_op jit(solution)/shard_map/ppermute | solution.py:160
  79.4 5.2 %collective-permute-start.14 = (bf16[288,256]{1,0:T(8,128)(2,1)S(1)}, bf16[288,256]{1,0:T(8,128)(2,1)S(1)}, u32[]{:S(2)}, u32[]{:S(2)}) collective-permute-start(bf16[288,256]{1,0:T(8,128)(2,1)S(1)} %dynamic-slice_convert_fusion.2), channel_id=1, source_target_pairs={{0,16},{1,17},{2,18},{3,19},{4,12},{5,13},{6,14},{7,15},{8,24},{9,... | collective-permute-start | bytes 442376 | tf_op jit(solution)/shard_map/ppermute | solution.py:160
  82.5 7.5 %collective-permute-start.8 = (bf16[288,256]{1,0:T(8,128)(2,1)S(1)}, bf16[288,256]{1,0:T(8,128)(2,1)S(1)}, u32[]{:S(2)}, u32[]{:S(2)}) collective-permute-start(bf16[288,256]{1,0:T(8,128)(2,1)S(1)} %add_convert_fusion.4), channel_id=1, source_target_pairs={{0,2},{1,3},{2,0},{3,1},{4,6},{5,7},{6,4},{7,5},{8,10},{9,11},{10,... | collective-permute-start | bytes 442376 | tf_op jit(solution)/shard_map/ppermute | solution.py:160
  84.7 7.3 %collective-permute-start.15 = (bf16[288,256]{1,0:T(8,128)(2,1)S(1)}, bf16[288,256]{1,0:T(8,128)(2,1)S(1)}, u32[]{:S(2)}, u32[]{:S(2)}) collective-permute-start(bf16[288,256]{1,0:T(8,128)(2,1)S(1)} %add_convert_fusion.2), channel_id=1, source_target_pairs={{0,1},{1,0},{2,3},{3,2},{4,5},{5,4},{6,7},{7,6},{8,9},{9,8},{10,11... | collective-permute-start | bytes 442376 | tf_op jit(solution)/shard_map/ppermute | solution.py:160
  90.0 6.8 %collective-permute-start.9 = (bf16[288,256]{1,0:T(8,128)(2,1)S(1)}, bf16[288,256]{1,0:T(8,128)(2,1)S(1)}, u32[]{:S(2)}, u32[]{:S(2)}) collective-permute-start(bf16[288,256]{1,0:T(8,128)(2,1)S(1)} %add_convert_fusion.3), channel_id=1, source_target_pairs={{0,16},{1,17},{2,18},{3,19},{4,12},{5,13},{6,14},{7,15},{8,24},{9,... | collective-permute-start | bytes 442376 | tf_op jit(solution)/shard_map/ppermute | solution.py:160
  92.1 7.7 %collective-permute-start.16 = (bf16[288,256]{1,0:T(8,128)(2,1)S(1)}, bf16[288,256]{1,0:T(8,128)(2,1)S(1)}, u32[]{:S(2)}, u32[]{:S(2)}) collective-permute-start(bf16[288,256]{1,0:T(8,128)(2,1)S(1)} %add_convert_fusion.1), channel_id=1, source_target_pairs={{0,2},{1,3},{2,0},{3,1},{4,6},{5,7},{6,4},{7,5},{8,10},{9,11},{10,... | collective-permute-start | bytes 442376 | tf_op jit(solution)/shard_map/ppermute | solution.py:160
  97.0 10.5 %collective-permute-start.10 = (bf16[576,256]{1,0:T(8,128)(2,1)S(1)}, bf16[576,256]{1,0:T(8,128)(2,1)S(1)}, u32[]{:S(2)}, u32[]{:S(2)}) collective-permute-start(bf16[576,256]{1,0:T(8,128)(2,1)S(1)} %maximum_select_fusion.4), channel_id=1, source_target_pairs={{0,8},{1,9},{2,10},{3,11},{4,20},{5,21},{6,22},{7,23},{8,0},{9,1},... | collective-permute-start | bytes 884744 | tf_op jit(solution)/shard_map/ppermute | solution.py:160
  99.8 6.3 %collective-permute-start.17 = (bf16[288,256]{1,0:T(8,128)(2,1)S(1)}, bf16[288,256]{1,0:T(8,128)(2,1)S(1)}, u32[]{:S(2)}, u32[]{:S(2)}) collective-permute-start(bf16[288,256]{1,0:T(8,128)(2,1)S(1)} %add_convert_fusion), channel_id=1, source_target_pairs={{0,16},{1,17},{2,18},{3,19},{4,12},{5,13},{6,14},{7,15},{8,24},{9,... | collective-permute-start | bytes 442376 | tf_op jit(solution)/shard_map/ppermute | solution.py:160
  106.2 6.8 %collective-permute-start.18 = (bf16[576,256]{1,0:T(8,128)(2,1)S(1)}, bf16[576,256]{1,0:T(8,128)(2,1)S(1)}, u32[]{:S(2)}, u32[]{:S(2)}) collective-permute-start(bf16[576,256]{1,0:T(8,128)(2,1)S(1)} %maximum_select_fusion.5), channel_id=1, source_target_pairs={{0,8},{1,9},{2,10},{3,11},{4,20},{5,21},{6,22},{7,23},{8,0},{9,1},... | collective-permute-start | bytes 884744 | tf_op jit(solution)/shard_map/ppermute | solution.py:160
  107.7 5.7 %collective-permute-start.11 = (bf16[1152,256]{1,0:T(8,128)(2,1)S(1)}, bf16[1152,256]{1,0:T(8,128)(2,1)S(1)}, u32[]{:S(2)}, u32[]{:S(2)}) collective-permute-start(bf16[1152,256]{1,0:T(8,128)(2,1)S(1)} %maximum_select_fusion.2), channel_id=1, source_target_pairs={{0,4},{1,5},{2,6},{3,7},{4,0},{5,1},{6,2},{7,3},{8,12},{9,13},{10,... | collective-permute-start | bytes 1769480 | tf_op jit(solution)/shard_map/ppermute | solution.py:160
  113.3 2.1 %collective-permute-start.19 = (bf16[1152,256]{1,0:T(8,128)(2,1)S(1)}, bf16[1152,256]{1,0:T(8,128)(2,1)S(1)}, u32[]{:S(2)}, u32[]{:S(2)}) collective-permute-start(bf16[1152,256]{1,0:T(8,128)(2,1)S(1)} %maximum_select_fusion.3), channel_id=1, source_target_pairs={{0,4},{1,5},{2,6},{3,7},{4,0},{5,1},{6,2},{7,3},{8,12},{9,13},{10,... | collective-permute-start | bytes 1769480 | tf_op jit(solution)/shard_map/ppermute | solution.py:160
